TPU v7x, 32 devices: a whole 2x2x4 slice. The times are simulated.
32 devices in a mesh: ctx: 8 (over z, x), tp: 4 (over y, core).
Axes of the slice: x: 2, y: 2, z: 4, core: 2. Of those that a mesh axis runs over, the one named last changes fastest.
Arguments:
- queries: bfloat16 [4096, 2048], P('ctx', 'tp'), may hold values from -40 to 40
- keys: bfloat16 [4096, 2048], P('ctx', 'tp'), may hold values from -40 to 40
- values: bfloat16 [4096, 2048], P('ctx', 'tp'), may hold values from -6 to 6
- out_weight: bfloat16 [2048, 4096], P('tp'), may hold values from -0.1875 to 0.1875
- doc_lengths: int32 [16], replicated, may hold values from 1 to 2048, 4096 in all
- layout: int32 [16], replicated, may hold values from 0 to 15, each once
Outputs:
- mixed: bfloat16 [4096, 4096], P('ctx', 'tp')
- log_totals: float32 [16, 4096], P('tp', 'ctx')
Inputs may be any that keep to these rules, and one draw needn't show every extreme that they name: `layout`: every block number appears once. `doc_lengths`: the lengths sum to 4096; the longest is exactly 2048.
All inputs are finite; a program needn't handle non-finite values.
Results may differ from a plain program's by a relative error of at most 0.012.
Values may be sent and summed in bfloat16 or wider, within the bound.
No kernel may reach another device: no remote copies, remote signals or barrier semaphores. Data moves between devices by JAX's collectives and lax.ppermute only.
A program may use at most 192 MiB of HBM per device.

v0:
```python
import math
import jax
import jax.numpy as jnp
from jax import lax
from jax.sharding import PartitionSpec as P

HEAD_DIM = 128


def positions_of(layout, first_row, count, half):
    rows = first_row + jnp.arange(count, dtype=jnp.int32)
    block_ids = rows // half
    table = jnp.arange(layout.shape[0], dtype=jnp.int32)
    owner = jnp.sum(jnp.where(block_ids[:, None] == table[None, :], layout[None, :], 0), axis=1)
    return owner * half + rows % half


def documents_of(starts, position):
    return jnp.sum((starts[None, :] <= position[:, None]).astype(jnp.int32), axis=1) - 1


def local(queries, keys, values, out_weight, doc_lengths, layout):
    rows = queries.shape[0]
    half = rows // 2
    heads = queries.shape[1] // HEAD_DIM
    scale = 1.0 / math.sqrt(HEAD_DIM)
    starts = jnp.cumsum(doc_lengths) - doc_lengths
    query_pos = positions_of(layout, lax.axis_index("ctx") * rows, rows, half)
    query_doc = documents_of(starts, query_pos)
    query_heads = queries.reshape(rows, heads, HEAD_DIM)

    def update(carry, key_blk, value_blk, allowed):
        top, totals, summed = carry
        scores = (
            jnp.einsum("qhd,khd->hqk", query_heads, key_blk, preferred_element_type=jnp.float32)
            * scale
        )
        scores = jnp.where(allowed[None], scores, -1e30)
        new_top = jnp.maximum(top, jnp.max(scores, axis=-1))
        weights = jnp.where(allowed[None], jnp.exp(scores - new_top[..., None]), 0.0)
        factor = jnp.exp(top - new_top)
        totals = totals * factor + jnp.sum(weights, axis=-1)
        summed = summed * factor.T[:, :, None] + jnp.einsum(
            "hqk,khd->qhd",
            weights.astype(jnp.bfloat16),
            value_blk,
            preferred_element_type=jnp.float32,
        )
        return (new_top, totals, summed)

    def tile(state, key_blk, value_blk, key_pos):
        key_doc = documents_of(starts, key_pos)
        allowed = (key_doc[None, :] == query_doc[:, None]) & (
            key_pos[None, :] <= query_pos[:, None]
        )
        return lax.cond(
            jnp.any(allowed),
            lambda inner: update(inner, key_blk, value_blk, allowed),
            lambda inner: inner,
            state,
        )

    initial = (
        jnp.full((heads, rows), -1e30, jnp.float32),
        jnp.zeros((heads, rows), jnp.float32),
        jnp.zeros((rows, heads, HEAD_DIM), jnp.float32),
    )
    key_piece = lax.all_gather(keys, "ctx", axis=0, tiled=True)
    value_piece = lax.all_gather(values, "ctx", axis=0, tiled=True)
    count = key_piece.shape[0]
    width = math.gcd(count, 512)

    def one_step(index, state):
        first = index * width
        key_blk = lax.dynamic_slice_in_dim(key_piece, first, width, 0).reshape(
            width, heads, HEAD_DIM
        )
        value_blk = lax.dynamic_slice_in_dim(value_piece, first, width, 0).reshape(
            width, heads, HEAD_DIM
        )
        key_pos = positions_of(layout, first, width, half)
        return tile(state, key_blk, value_blk, key_pos)

    top, totals, summed = lax.fori_loop(0, count // width, one_step, initial)
    attended = (summed / totals.T[:, :, None]).reshape(rows, heads * HEAD_DIM).astype(jnp.bfloat16)
    log_totals = top + jnp.log(totals)
    partial_value = jnp.dot(attended, out_weight, preferred_element_type=jnp.float32)
    mixed = lax.psum_scatter(
        partial_value.astype(jnp.bfloat16), "tp", scatter_dimension=1, tiled=True
    )
    return (mixed, log_totals)


def solution(mesh):
    placed = (P("ctx", "tp"), P("ctx", "tp"), P("ctx", "tp"), P("tp", None), P(), P())
    return jax.shard_map(
        local,
        mesh=mesh,
        in_specs=placed,
        out_specs=(P("ctx", "tp"), P("tp", "ctx")),
        check_vma=False,
    )
```

profile of v0, /device:TPU:0, one launch (start us, length us, event | category | flops | bytes accessed | tf_op | source)
XLA Modules:
  0.0 267.7 jit_solution(391481774716480319)
XLA Ops:
  7.2 0.0 copy-start
  7.2 0.0 all-gather.3.cloned.1.call-start
  7.2 2.0 copy.23
  9.3 0.0 all-gather.3.cloned.1.call-update
  9.3 0.0 all-gather.5.cloned.1.call-start
  9.3 2.1 copy.25
  11.4 0.0 all-gather.5.cloned.1.call-update
  11.5 0.0 reduce-scatter.2.cloned.1.call-start
  11.5 0.7 copy.22
  12.3 0.1 reduce
  12.4 0.7 sub.45
  13.1 1.3 copy.24
  14.3 0.3 copy.26
  14.6 0.0 copy-done
  14.6 0.1 select_reduce_fusion.1
  14.7 0.1 convert_reduce_fusion.1
  14.8 73.2 %all-gather.3.cloned.1.call-done = bf16[4096,512]{0,1:T(8,128)(2,1)} async-done(((bf16[512,512]{0,1:T(8,128)(2,1)}), bf16[4096,512]{0,1:T(8,128)(2,1)}) %all-gather.3.cloned.1.call-update) | async-done | bytes 4194320 | tf_op jit(solution)/shard_map/all_gather | solution.py:68
  88.0 74.9 %all-gather.5.cloned.1.call-done = bf16[4096,512]{0,1:T(8,128)(2,1)} async-done(((bf16[512,512]{0,1:T(8,128)(2,1)}), bf16[4096,512]{0,1:T(8,128)(2,1)}) %all-gather.5.cloned.1.call-update) | async-done | bytes 4194320 | tf_op jit(solution)/shard_map/all_gather | solution.py:69
  162.9 0.1 broadcast_in_dim.115
  163.0 24.4 %while.20 = (s32[]{:T(128)}, f32[4,512]{1,0:T(4,128)S(1)}, f32[4,512]{1,0:T(4,128)S(1)}, f32[512,4,128]{2,0,1:T(8,128)S(1)}, s32[16]{0:T(128)S(1)}, /*index=5*/s...) while((s32[]{:T(128)}, f32[4,512]{1,0:T(4,128)S(1)}, ...), condition=%wide.region_11.12_spmd, body=%wide.region_3.11_spmd.sunk | while | flops 552145408 | bytes 19556788 | solution.py:84
  163.0 0.1 select_reduce_fusion.3
  163.1 0.1 convert_reduce_fusion.3
  163.2 0.9 fusion.33
  164.7 5.2 %conditional.2 = ((f32[4,512]{1,0:T(4,128)S(1)}, f32[4,512]{1,0:T(4,128)S(1)}, f32[512,4,128]{2,0,1:T(8,128)S(1)})) conditional(s32[]{:T(128)} %convert_element_type.57, (f32[4,512]{1,0:T(4,128)S(1)}, f32[4,512]{1,0:T(4,128)S(1)}, f32[512,4,128]{2,0,1:T(8,128)S(1)}) %tuple.70, (pred[512,512]{0,1:T(8,128)(4,1)S(1)}, s32[]{:T(128)}, ...), branch_computations={%region_7.7_spmd, %region_8.10_spmd} | conditional | flops 551032832 | bytes 19267654 | solution.py:56
  164.7 1.3 constant_dynamic-slice_fusion
  166.0 1.0 fusion
  167.0 1.8 fusion.9
  168.8 1.0 fusion.2
  169.9 0.1 select_reduce_fusion.3
  170.1 0.1 convert_reduce_fusion.3
  170.1 0.9 fusion.33
  171.7 0.1 select_reduce_fusion.3
  171.8 0.1 convert_reduce_fusion.3
  171.9 0.9 fusion.33
  173.4 0.1 select_reduce_fusion.3
  173.5 0.1 convert_reduce_fusion.3
  173.6 0.9 fusion.33
  175.2 0.1 select_reduce_fusion.3
  175.3 0.1 convert_reduce_fusion.3
  175.4 0.9 fusion.33
  176.9 0.1 select_reduce_fusion.3
  177.0 0.1 convert_reduce_fusion.3
  177.1 0.9 fusion.33
  178.6 5.2 %conditional.2 = ((f32[4,512]{1,0:T(4,128)S(1)}, f32[4,512]{1,0:T(4,128)S(1)}, f32[512,4,128]{2,0,1:T(8,128)S(1)})) conditional(s32[]{:T(128)} %convert_element_type.57, (f32[4,512]{1,0:T(4,128)S(1)}, f32[4,512]{1,0:T(4,128)S(1)}, f32[512,4,128]{2,0,1:T(8,128)S(1)}) %tuple.70, (pred[512,512]{0,1:T(8,128)(4,1)S(1)}, s32[]{:T(128)}, ...), branch_computations={%region_7.7_spmd, %region_8.10_spmd} | conditional | flops 551032832 | bytes 19267654 | solution.py:56
  178.6 1.3 constant_dynamic-slice_fusion
  179.9 1.0 fusion
  181.0 1.8 fusion.9
  182.8 1.0 fusion.2
  183.9 0.1 select_reduce_fusion.3
  184.0 0.1 convert_reduce_fusion.3
  184.1 0.9 fusion.33
  185.6 0.1 select_reduce_fusion.3
  185.7 0.1 convert_reduce_fusion.3
  185.8 0.9 fusion.33
  187.3 0.3 copy.27
  187.7 0.1 divide_convert_fusion
  187.8 6.5 %convolution_convert_fusion = bf16[512,4096]{1,0:T(8,128)(2,1)} fusion(bf16[512,512]{0,1:T(8,128)(2,1)S(1)} %bitcast.34, bf16[512,4096]{1,0:T(8,128)(2,1)} %param.13), kind=kOutput, calls=%fused_computation.33 | convolution fusion | flops 2149580800 | bytes 8912896 | tf_op jit(solution)/shard_map/dot_general | solution.py:87
  194.3 0.0 reduce-scatter.2.cloned.1.call-update
  194.3 0.6 log_add_fusion
  194.9 66.3 %reduce-scatter.2.cloned.1.call-done = bf16[512,1024]{1,0:T(8,128)(2,1)} async-done(((bf16[512,4096]{1,0:T(8,128)(2,1)}), bf16[512,1024]{1,0:T(8,128)(2,1)}) %reduce-scatter.2.cloned.1.call-update) | async-done | bytes 1048592 | tf_op jit(solution)/shard_map/reduce_scatter | solution.py:88
  (42 shorter events, 0.5 us)
Async XLA Ops:
  7.2 7.5 %copy-start = (s32[16]{0:T(128)S(1)}, s32[16]{0:T(128)}, u32[]{:S(2)}) copy-start(s32[16]{0:T(128)} %param.15) | copy-start | bytes 196
  7.2 80.8 %all-gather.3.cloned.1.call-start = ((), (), s32[]{:S(2)}) async-start(), calls=%async_computation.1 | async-start | bytes 4718592 | tf_op jit(solution)/shard_map/all_gather | solution.py:68
  9.3 153.6 %all-gather.5.cloned.1.call-start = ((), (), s32[]{:S(2)}) async-start(), calls=%async_computation.2 | async-start | bytes 4718592 | tf_op jit(solution)/shard_map/all_gather | solution.py:69
  11.5 249.7 %reduce-scatter.2.cloned.1.call-start = ((), (), s32[]{:S(2)}) async-start(), calls=%async_computation.3 | async-start | bytes 5242880 | tf_op jit(solution)/shard_map/reduce_scatter | solution.py:88
Sparse Core Ops, SparseCore 0:
  10.6 77.3 all-gather.2
  90.0 72.8 all-gather.4
  194.5 66.7 reduce-scatter.1
where the time goes:
time: 268 us
  waiting for transfers between devices  214 us (80%)
  between operations  13.8 us (5%)
  other arithmetic  12.9 us (5%)
  matrix products  12.1 us (5%)
  local copies, waits for them, and re-layouts  9.37 us (3%)
  loops' own time  5.08 us (2%)
    all_gather x1, waiting for transfers between devices, local(): value_piece = lax.all_gather(values, 'ctx', axis=0, tiled=True)  74.9 us
    all_gather x1, waiting for transfers between devices, local(): key_piece = lax.all_gather(keys, 'ctx', axis=0, tiled=True)  73.2 us
    reduce_scatter x1, waiting for transfers between devices, local(): lax.psum_scatter(partial_value.astype(jnp.bfloat16), 'tp', scatter_dimens...  66.3 us
    reduce_or x8, other arithmetic, tile(): jnp.any(allowed)  7.31 us
    dot_general x1, matrix products, local(): jnp.dot(attended, out_weight, preferred_element_type=jnp.float32)  6.49 us
    unnamed x5, local copies, waits for them, and re-layouts  5.4 us
  transfers between devices with their start and end apart: 3, of which 3 were waited for; matrix products, arithmetic and copies ran while one was open for 2% of the time, Pallas kernels for 0%

commit v1 on v0

--- a/solution.py
+++ b/solution.py
@@ -65,8 +65,11 @@
         jnp.zeros((heads, rows), jnp.float32),
         jnp.zeros((rows, heads, HEAD_DIM), jnp.float32),
     )
-    key_piece = lax.all_gather(keys, "ctx", axis=0, tiled=True)
-    value_piece = lax.all_gather(values, "ctx", axis=0, tiled=True)
+    key_piece, value_piece = jnp.split(
+        lax.all_gather(jnp.concatenate([keys, values], axis=1), "ctx", axis=0, tiled=True),
+        [keys.shape[1]],
+        axis=1,
+    )
     count = key_piece.shape[0]
     width = math.gcd(count, 512)
 

time: 268 us -> 252 us (0.940)
  waiting for transfers between devices: 214 us -> 193 us
    all_gather x2 -> x1, waiting for transfers between devices: 148 us -> 127 us  [local(): lax.all_gather(jnp.concatenate([keys, values], axis=1), 'ctx', axis=0, ti...]
    split x0 -> x1, local copies, waits for them, and re-layouts: none -> 5.93 us  [local(): jnp.split(lax.all_gather(jnp.concatenate([keys, values], axis=1), 'ctx',...]
    unnamed x5 -> x9, local copies, waits for them, and re-layouts: 5.4 us -> 2.78 us
  transfers between devices with their start and end apart: 3 -> 2, of which waited for: 3 -> 2; matrix products, arithmetic and copies ran while one was open for 2% -> 1% of each run, Pallas kernels for 0% -> 0%
where the time goes in v1:
time: 252 us
  waiting for transfers between devices  193 us (77%)
  between operations  14.2 us (6%)
  other arithmetic  14.1 us (6%)
  matrix products  12.1 us (5%)
  local copies, waits for them, and re-layouts  12 us (5%)
  loops' own time  6.05 us (2%)
    all_gather x1, waiting for transfers between devices, local(): lax.all_gather(jnp.concatenate([keys, values], axis=1), 'ctx', axis=0, ti...  127 us
    reduce_scatter x1, waiting for transfers between devices, local(): lax.psum_scatter(partial_value.astype(jnp.bfloat16), 'tp', scatter_dimens...  66.3 us
    reduce_or x8, other arithmetic, tile(): jnp.any(allowed)  8.17 us
    dot_general x1, matrix products, local(): jnp.dot(attended, out_weight, preferred_element_type=jnp.float32)  6.49 us
    split x1, local copies, waits for them, and re-layouts, local(): jnp.split(lax.all_gather(jnp.concatenate([keys, values], axis=1), 'ctx',...  5.93 us
    another operation x1, loops' own time, local(): top, totals, summed = lax.fori_loop(0, count // width, one_step, initial)  5.84 us
  transfers between devices with their start and end apart: 2, of which 2 were waited for; matrix products, arithmetic and copies ran while one was open for 1% of the time, Pallas kernels for 0%

profile of v1, /device:TPU:0, one launch (start us, length us, event | category | flops | bytes accessed | tf_op | source)
XLA Modules:
  0.0 251.6 jit_solution(9716304159598562979)
XLA Ops:
  7.2 0.0 copy-start.2
  7.2 0.0 copy-start
  7.2 0.0 copy-start.1
  7.2 0.0 all-gather.2.cloned.1.call-start
  7.2 1.3 copy.23
  8.5 1.3 copy.24
  9.8 1.0 pad_maximum_fusion
  10.8 0.0 all-gather.2.cloned.1.call-update
  10.9 0.0 reduce-scatter.2.cloned.1.call-start
  10.9 0.0 copy-done.2
  10.9 0.1 copy.22
  11.1 0.1 reduce
  11.2 0.0 copy-done
  11.2 0.2 copy.25
  11.4 0.3 copy.26
  11.7 0.0 copy-done.1
  11.7 0.1 select_reduce_fusion.1
  11.8 0.1 convert_reduce_fusion.1
  11.9 126.8 %all-gather.2.cloned.1.call-done = bf16[4096,1024]{0,1:T(8,128)(2,1)} async-done(((bf16[512,1024]{0,1:T(8,128)(2,1)}), bf16[4096,1024]{0,1:T(8,128)(2,1)}) %all-gather.2.cloned.1.call-update) | async-done | bytes 8388624 | tf_op jit(solution)/shard_map/all_gather | solution.py:69
  138.7 5.9 %fusion.25 = (bf16[4096,512]{0,1:T(8,128)(2,1)}, bf16[4096,512]{0,1:T(8,128)(2,1)}) fusion(bf16[4096,1024]{0,1:T(8,128)(2,1)} %all-gather.2.cloned.1.call-done), kind=kLoop, calls=%fused_computation.53 | loop fusion | bytes 16777216 | tf_op jit(solution)/shard_map/split | solution.py:68
  144.6 0.1 broadcast_in_dim.115
  144.7 26.2 %while.20 = (s32[]{:T(128)}, f32[4,512]{1,0:T(4,128)S(1)}, f32[4,512]{1,0:T(4,128)S(1)}, f32[512,4,128]{2,0,1:T(8,128)S(1)}, s32[16]{0:T(128)S(1)}, /*index=5*/s...) while((s32[]{:T(128)}, f32[4,512]{1,0:T(4,128)S(1)}, ...), condition=%wide.region_11.12_spmd, body=%wide.region_3.11_spmd.sunk | while | flops 552145408 | bytes 19556788 | solution.py:87
  144.7 0.1 select_reduce_fusion.3
  144.8 0.1 convert_reduce_fusion.3
  144.9 1.0 fusion.34
  146.7 5.2 %conditional.2 = ((f32[4,512]{1,0:T(4,128)S(1)}, f32[4,512]{1,0:T(4,128)S(1)}, f32[512,4,128]{2,0,1:T(8,128)S(1)})) conditional(s32[]{:T(128)} %convert_element_type.57, (f32[4,512]{1,0:T(4,128)S(1)}, f32[4,512]{1,0:T(4,128)S(1)}, f32[512,4,128]{2,0,1:T(8,128)S(1)}) %tuple.71, (pred[512,512]{0,1:T(8,128)(4,1)S(1)}, s32[]{:T(128)}, ...), branch_computations={%region_7.7_spmd, %region_8.10_spmd} | conditional | flops 551032832 | bytes 19267654 | solution.py:56
  146.7 1.3 constant_dynamic-slice_fusion
  148.0 1.0 fusion
  149.0 1.8 fusion.9
  150.8 1.0 fusion.2
  151.9 0.1 select_reduce_fusion.3
  152.0 0.1 convert_reduce_fusion.3
  152.1 1.0 fusion.34
  153.9 0.1 select_reduce_fusion.3
  154.0 0.1 convert_reduce_fusion.3
  154.1 1.0 fusion.34
  155.9 0.1 select_reduce_fusion.3
  156.0 0.1 convert_reduce_fusion.3
  156.1 1.0 fusion.34
  157.8 0.1 select_reduce_fusion.3
  157.9 0.1 convert_reduce_fusion.3
  158.0 1.0 fusion.34
  159.8 0.1 select_reduce_fusion.3
  159.9 0.1 convert_reduce_fusion.3
  160.0 1.0 fusion.34
  161.7 5.2 %conditional.2 = ((f32[4,512]{1,0:T(4,128)S(1)}, f32[4,512]{1,0:T(4,128)S(1)}, f32[512,4,128]{2,0,1:T(8,128)S(1)})) conditional(s32[]{:T(128)} %convert_element_type.57, (f32[4,512]{1,0:T(4,128)S(1)}, f32[4,512]{1,0:T(4,128)S(1)}, f32[512,4,128]{2,0,1:T(8,128)S(1)}) %tuple.71, (pred[512,512]{0,1:T(8,128)(4,1)S(1)}, s32[]{:T(128)}, ...), branch_computations={%region_7.7_spmd, %region_8.10_spmd} | conditional | flops 551032832 | bytes 19267654 | solution.py:56
  161.8 1.3 constant_dynamic-slice_fusion
  163.0 1.0 fusion
  164.1 1.8 fusion.9
  165.9 1.0 fusion.2
  167.0 0.1 select_reduce_fusion.3
  167.1 0.1 convert_reduce_fusion.3
  167.2 1.0 fusion.34
  169.0 0.1 select_reduce_fusion.3
  169.1 0.1 convert_reduce_fusion.3
  169.2 1.0 fusion.34
  170.9 0.3 copy.27
  171.3 0.1 divide_convert_fusion
  171.4 6.5 %convolution_convert_fusion = bf16[512,4096]{1,0:T(8,128)(2,1)} fusion(bf16[512,512]{0,1:T(8,128)(2,1)S(1)} %bitcast.34, bf16[512,4096]{1,0:T(8,128)(2,1)} %param.13), kind=kOutput, calls=%fused_computation.33 | convolution fusion | flops 2149580800 | bytes 8912896 | tf_op jit(solution)/shard_map/dot_general | solution.py:90
  177.9 0.0 reduce-scatter.2.cloned.1.call-update
  177.9 0.6 log_add_fusion
  178.5 66.3 %reduce-scatter.2.cloned.1.call-done = bf16[512,1024]{1,0:T(8,128)(2,1)} async-done(((bf16[512,4096]{1,0:T(8,128)(2,1)}), bf16[512,1024]{1,0:T(8,128)(2,1)}) %reduce-scatter.2.cloned.1.call-update) | async-done | bytes 1048592 | tf_op jit(solution)/shard_map/reduce_scatter | solution.py:91
  (43 shorter events, 0.5 us)
Async XLA Ops:
  7.2 3.8 %copy-start.2 = (s32[16]{0:T(128)S(1)}, s32[16]{0:T(128)}, u32[]{:S(2)}) copy-start(s32[16]{0:T(128)} %param.14) | copy-start | bytes 196
  7.2 4.0 %copy-start = (bf16[512,512]{1,0:T(8,128)(2,1)S(1)}, bf16[512,512]{1,0:T(8,128)(2,1)}, u32[]{:S(2)}) copy-start(bf16[512,512]{1,0:T(8,128)(2,1)} %param.10) | copy-start | bytes 1572868
  7.2 4.5 %copy-start.1 = (s32[16]{0:T(128)S(1)}, s32[16]{0:T(128)}, u32[]{:S(2)}) copy-start(s32[16]{0:T(128)} %param.15) | copy-start | bytes 196
  7.2 131.5 %all-gather.2.cloned.1.call-start = ((), (), s32[]{:S(2)}) async-start(), calls=%async_computation.1 | async-start | bytes 9437184 | tf_op jit(solution)/shard_map/all_gather | solution.py:69
  10.9 233.9 %reduce-scatter.2.cloned.1.call-start = ((), (), s32[]{:S(2)}) async-start(), calls=%async_computation.2 | async-start | bytes 5242880 | tf_op jit(solution)/shard_map/reduce_scatter | solution.py:91
Sparse Core Ops, SparseCore 0:
  11.0 127.6 all-gather.1
  178.0 66.7 reduce-scatter.1
